TPU v7x, 128 devices: a whole 4x4x4 slice. The times are simulated.
128 devices in a mesh: blk: 16 (over z, x_hi, core), uly: 8 (over y, x_lo).
Axes of the slice: x: 4 (x_hi: 2, x_lo: 2; x = x_hi * 2 + x_lo), y: 4, z: 4, core: 2. Of those that a mesh axis runs over, the one named last changes fastest.
Arguments:
- queries: bfloat16 [2048, 128, 128], P(('blk', 'uly')), may hold values from -8 to 8
- query_tangents: bfloat16 [2048, 128, 4, 128], P(('blk', 'uly')), may hold values from -6 to 6
- keys: bfloat16 [2048, 8, 128], P(('blk', 'uly')), may hold values from -8 to 8
- key_tangents: bfloat16 [2048, 8, 4, 128], P(('blk', 'uly')), may hold values from -6 to 6
- values: bfloat16 [2048, 8, 128], P(('blk', 'uly')), may hold values from -6 to 6
- value_tangents: bfloat16 [2048, 8, 4, 128], P(('blk', 'uly')), may hold values from -6 to 6
- span_order: int32 [32], replicated, may hold values from 0 to 31, as said below
Outputs:
- attention_out: bfloat16 [2048, 128, 128], P(('blk', 'uly'))
- tangent_out: bfloat16 [2048, 128, 4, 128], P(('blk', 'uly'))
Inputs may be any that keep to these rules, and one draw needn't show every extreme that they name: span_order is a permutation of the span positions; for every b the stored spans 2 * b and 2 * b + 1 hold positions c and 31 - c for some c.
All inputs are finite; a program needn't handle non-finite values.
Results may differ from a plain program's by a relative error of at most 0.0055.
Values may be sent and summed in bfloat16 or wider, within the bound.
No kernel may reach another device: no remote copies, remote signals or barrier semaphores. Data moves between devices by JAX's collectives and lax.ppermute only.
A program may use at most 64 MiB of HBM per device.

v0:
```python
import math
import jax
import jax.numpy as jnp
from jax import lax
from jax.sharding import PartitionSpec as P

HQ = 128
KVH = 8


def in_one_piece(arrays, axis, split_dim, concat_dim, along):
    widths = [math.prod(a.shape[along:]) for a in arrays]
    both = jnp.concatenate(
        [a.reshape(*a.shape[:along], w) for a, w in zip(arrays, widths)], axis=along
    )
    out = lax.all_to_all(both, axis, split_axis=split_dim, concat_axis=concat_dim, tiled=True)
    parts = jnp.split(out, [sum(widths[:k]) for k in range(1, len(widths))], axis=along)
    return tuple((b.reshape(*out.shape[:along], *a.shape[along:]) for a, b in zip(arrays, parts)))


def sent_together(arrays, axis, dim, along):
    columns = [a.reshape(*a.shape[:along], -1) for a in arrays]
    both = jnp.concatenate(columns, axis=along)
    out, at, finished = (lax.all_gather(both, axis, axis=dim, tiled=True), 0, [])
    for a, column in zip(arrays, columns):
        slab = out[..., at : at + column.shape[along]]
        finished.append(slab.reshape(*slab.shape[:along], *a.shape[along:]))
        at += column.shape[along]
    return tuple(finished)


def positions(stored, span_order, span_rows):
    span_ids = stored // span_rows
    table_ids = jnp.arange(span_order.shape[0], dtype=jnp.int32)
    looked_up = jnp.sum(
        jnp.where(span_ids[:, None] == table_ids[None, :], span_order[None, :], 0), axis=1
    )
    return looked_up * span_rows + stored % span_rows


def per_device(queries, query_tangents, keys, key_tangents, values, value_tangents, span_order):
    local_queries, local_tangents = (
        lax.all_to_all(queries, "uly", split_axis=1, concat_axis=0, tiled=True),
        lax.all_to_all(query_tangents, "uly", split_axis=1, concat_axis=0, tiled=True),
    )
    query_rows = local_queries.shape[0]
    span_rows = query_rows // 2
    head_size = local_queries.shape[2]
    group = HQ // KVH
    kv_local = local_queries.shape[1] // group
    probes = local_tangents.shape[2]
    scaling = head_size ** (-0.5)
    stored = lax.axis_index("blk") * query_rows + jnp.arange(query_rows, dtype=jnp.int32)
    query_places = positions(stored, span_order, span_rows)
    latest = jnp.max(query_places)
    query_heads = jnp.transpose(
        local_queries.reshape(query_rows, kv_local, group, head_size), (1, 2, 0, 3)
    )
    tangent_heads = jnp.transpose(
        local_tangents.reshape(query_rows, kv_local, group, probes, head_size), (1, 2, 3, 0, 4)
    )

    def update(carry, block):
        key_block, key_tan, value_block, value_tan, key_places = block
        running_max, totals, primal_sums, tangent_sums, shifts = carry
        visible = key_places[None, :] <= query_places[:, None]
        scores = (
            jnp.einsum("grqd,kgd->grqk", query_heads, key_block, preferred_element_type=jnp.float32)
            * scaling
        )
        scores = jnp.where(visible[None, None], scores, -1e30)
        new_max = jnp.maximum(running_max, jnp.max(scores, axis=-1))
        rescale = jnp.exp(running_max - new_max)
        weights_full = jnp.where(visible[None, None], jnp.exp(scores - new_max[..., None]), 0.0)
        weights_half = weights_full.astype(jnp.bfloat16)
        score_tan = jnp.einsum(
            "grpqd,kgd->grpqk", tangent_heads, key_block, preferred_element_type=jnp.float32
        )
        score_tan = score_tan + jnp.einsum(
            "grqd,kgpd->grpqk", query_heads, key_tan, preferred_element_type=jnp.float32
        )
        weighted = weights_full[:, :, None] * (score_tan * scaling)
        totals = totals * rescale + jnp.sum(weights_full, axis=-1)
        primal_sums = primal_sums * rescale[..., None] + jnp.einsum(
            "grqk,kgd->grqd", weights_half, value_block, preferred_element_type=jnp.float32
        )
        shifts = shifts * rescale[:, :, None] + jnp.sum(weighted, axis=-1)
        tangent_sums = tangent_sums * rescale[:, :, None, :, None]
        tangent_sums = tangent_sums + jnp.einsum(
            "grpqk,kgd->grpqd",
            weighted.astype(jnp.bfloat16),
            value_block,
            preferred_element_type=jnp.float32,
        )
        tangent_sums = tangent_sums + jnp.einsum(
            "grqk,kgpd->grpqd", weights_half, value_tan, preferred_element_type=jnp.float32
        )
        return (new_max, totals, primal_sums, tangent_sums, shifts)

    def keep_state(carry, block):
        return carry

    def visit(carry, block):
        reachable = jnp.min(block[4]) <= latest
        return (lax.cond(reachable, update, keep_state, carry, block), None)

    initial = (
        jnp.full((kv_local, group, query_rows), -1e30, jnp.float32),
        jnp.zeros((kv_local, group, query_rows), jnp.float32),
        jnp.zeros((kv_local, group, query_rows, head_size), jnp.float32),
        jnp.zeros((kv_local, group, probes, query_rows, head_size), jnp.float32),
        jnp.zeros((kv_local, group, probes, query_rows), jnp.float32),
    )
    head_keys, head_key_tan, head_values, head_value_tan = in_one_piece(
        (keys, key_tangents, values, value_tangents), "uly", 1, 0, 2
    )
    carry = initial
    key_piece, key_tan_piece, value_piece, value_tan_piece = sent_together(
        (head_keys, head_key_tan, head_values, head_value_tan), "blk", 0, 2
    )
    piece_rows = key_piece.shape[0]
    block_rows = 256
    block_total = piece_rows // block_rows
    places = positions(jnp.arange(piece_rows, dtype=jnp.int32), span_order, span_rows)
    stacked = (
        key_piece.reshape(block_total, block_rows, kv_local, head_size),
        key_tan_piece.reshape(block_total, block_rows, kv_local, probes, head_size),
        value_piece.reshape(block_total, block_rows, kv_local, head_size),
        value_tan_piece.reshape(block_total, block_rows, kv_local, probes, head_size),
        places.reshape(block_total, block_rows),
    )
    carry, unused = lax.scan(visit, carry, stacked)
    running_max, totals, primal_sums, tangent_sums, shifts = carry
    primal = primal_sums / totals[..., None]
    tangent = (
        tangent_sums / totals[:, :, None, :, None]
        - primal[:, :, None] * (shifts / totals[:, :, None])[..., None]
    )
    output_rows = jnp.transpose(primal.astype(jnp.bfloat16), (2, 0, 1, 3)).reshape(
        query_rows, kv_local * group, head_size
    )
    tangent_rows = jnp.transpose(tangent.astype(jnp.bfloat16), (3, 0, 1, 2, 4)).reshape(
        query_rows, kv_local * group, probes, head_size
    )
    attention_out, tangent_out = (
        lax.all_to_all(output_rows, "uly", split_axis=0, concat_axis=1, tiled=True),
        lax.all_to_all(tangent_rows, "uly", split_axis=0, concat_axis=1, tiled=True),
    )
    return (attention_out, tangent_out)


def solution(mesh):
    placed = (
        P(("blk", "uly"), None, None),
        P(("blk", "uly"), None, None, None),
        P(("blk", "uly"), None, None),
        P(("blk", "uly"), None, None, None),
        P(("blk", "uly"), None, None),
        P(("blk", "uly"), None, None, None),
        P(),
    )
    return jax.shard_map(
        per_device,
        mesh=mesh,
        in_specs=placed,
        out_specs=(P(("blk", "uly"), None, None), P(("blk", "uly"), None, None, None)),
        check_vma=False,
    )
```

profile of v0, /device:TPU:0, one launch (start us, length us, event | category | flops | bytes accessed | tf_op | source)
XLA Modules:
  0.0 317.2 jit_solution(10333332695281003336)
XLA Ops:
  11.0 13.5 %all_to_all.84 = bf16[16,8,1280]{2,0,1:T(8,128)(2,1)} all-to-all(bf16[16,8,1280]{2,0,1:T(8,128)(2,1)S(1)} %pad_maximum_fusion), channel_id=1, replica_groups=mesh['blk'=16,'uly'=8] {'uly'}, dimensions={1} | all-to-all | bytes 655360 | tf_op jit(solution)/shard_map/all_to_all | solution.py:16
  25.7 3.5 %all-to-all-start.1 = ((bf16[16,128,128]{2,0,1:T(8,128)(2,1)}), bf16[16,128,128]{2,0,1:T(8,128)(2,1)S(1)}, u32[]{:S(2)}, u32[]{:S(2)}) async-start(bf16[16,128,128]{2,0,1:T(8,128)(2,1)} %copy.87), calls=%async_computation.1 | async-start | bytes 1048576 | tf_op jit(solution)/shard_map/all_to_all | solution.py:43
  31.7 6.5 %all-to-all-done.1 = bf16[16,128,128]{2,0,1:T(8,128)(2,1)S(1)} async-done(((bf16[16,128,128]{2,0,1:T(8,128)(2,1)}), bf16[16,128,128]{2,0,1:T(8,128)(2,1)S(1)}, u32[]{:S(2)}, u32[]{:S(2)}) %all-to-all-start.1) | async-done | bytes 524320 | tf_op jit(solution)/shard_map/all_to_all | solution.py:43
  38.2 3.6 %all-to-all-start.2 = ((bf16[16,128,4,128]{3,2,0,1:T(4,128)(2,1)}), bf16[16,128,4,128]{3,2,0,1:T(4,128)(2,1)S(1)}, u32[]{:S(2)}, u32[]{:S(2)}) async-start(bf16[16,128,4,128]{3,2,0,1:T(4,128)(2,1)} %copy.89), calls=%async_computation.2 | async-start | bytes 4194304 | tf_op jit(solution)/shard_map/all_to_all | solution.py:44
  42.9 32.5 %all-to-all-done.2 = bf16[16,128,4,128]{3,2,0,1:T(4,128)(2,1)S(1)} async-done(((bf16[16,128,4,128]{3,2,0,1:T(4,128)(2,1)}), bf16[16,128,4,128]{3,2,0,1:T(4,128)(2,1)S(1)}, u32[]{:S(2)}, u32[]{:S(2)}) %all-to-all-start.2) | async-done | bytes 2097184 | tf_op jit(solution)/shard_map/all_to_all | solution.py:44
  78.9 11.5 %all-gather.2.cloned.1.call-done = bf16[2048,1,1280]{2,0,1:T(8,128)(2,1)} async-done(((bf16[128,1,1280]{2,0,1:T(8,128)(2,1)}), bf16[2048,1,1280]{2,0,1:T(8,128)(2,1)}) %all-gather.2.cloned.1.call-update) | async-done | bytes 5242896 | tf_op jit(solution)/shard_map/all_gather | solution.py:24
  90.5 4.6 %fusion.48 = (bf16[2048,1,512]{2,0,1:T(8,128)(2,1)}, bf16[2048,1,512]{2,0,1:T(8,128)(2,1)}) fusion(bf16[2048,1,1280]{2,0,1:T(8,128)(2,1)} %all-gather.2.cloned.1.call-done), kind=kLoop, calls=%fused_computation.81 | loop fusion | bytes 8388608 | tf_op jit(solution)/shard_map/slice | solution.py:26
  95.1 4.0 %reshape.242 = bf16[8,256,1,4,128]{4,3,1,0,2:T(4,128)(2,1)} reshape(bf16[2048,1,512]{2,0,1:T(8,128)(2,1)} %get-tuple-element.325) | data formatting | bytes 4194304 | tf_op jit(solution)/shard_map/reshape;reshape | solution.py:129
  99.0 4.2 %copy.96 = bf16[8,256,1,4,128]{1,4,3,2,0:T(8,128)(2,1)} copy(bf16[8,256,1,4,128]{4,3,1,0,2:T(4,128)(2,1)} %reshape.242) | data formatting | bytes 4194304 | tf_op jit(solution)/shard_map/while | solution.py:132
  103.2 4.0 %reshape.241 = bf16[8,256,1,4,128]{4,3,1,0,2:T(4,128)(2,1)} reshape(bf16[2048,1,512]{2,0,1:T(8,128)(2,1)} %get-tuple-element.326) | data formatting | bytes 4194304 | tf_op jit(solution)/shard_map/reshape;reshape | solution.py:127
  107.2 3.5 %copy.95 = bf16[8,256,1,4,128]{4,1,3,2,0:T(8,128)(2,1)} copy(bf16[8,256,1,4,128]{4,3,1,0,2:T(4,128)(2,1)} %reshape.241) | data formatting | bytes 4194304 | tf_op jit(solution)/shard_map/while | solution.py:132
  116.3 142.2 %while.18 = (s32[]{:T(128)}, f32[1,16,128]{2,1,0:T(8,128)S(1)}, f32[1,16,128]{2,1,0:T(8,128)S(1)}, f32[1,16,128,128]{3,2,1,0:T(8,128)}, f32[1,16,4,128,128]{4,3,...) while((s32[]{:T(128)}, f32[1,16,128]{2,1,0:T(8,128)S(1)}, ...), condition=%wide.region_10.11_spmd, body=%wide.region_3.10_spmd.sunk | while | flops 2437986560 | bytes 102954992 | solution.py:132
  118.4 15.7 %conditional.2 = ((f32[1,16,128]{2,1,0:T(8,128)S(1)}, f32[1,16,128]{2,1,0:T(8,128)S(1)}, f32[1,16,128,128]{3,2,1,0:T(8,128)}, f32[1,16,4,128,128]{4,3,2,1,0:T(8,128)}, f32[1,16,4,128]{3,2,1,0:T(4,128)S(1)})) conditional(s32[]{:T(128)} %convert_element_type.36, (f32[1,16,128]{2,1,0:T(8,128)S(1)}, f32[1,16,128]{2,1,0:T(8,128)S(1)}, ...), branch_computations={%region_5.5_spmd, %region_6.9_spmd} | conditional | flops 2437986304 | bytes 102952616 | solution.py:105
  136.2 15.7 %conditional.2 = ((f32[1,16,128]{2,1,0:T(8,128)S(1)}, f32[1,16,128]{2,1,0:T(8,128)S(1)}, f32[1,16,128,128]{3,2,1,0:T(8,128)}, f32[1,16,4,128,128]{4,3,2,1,0:T(8,128)}, f32[1,16,4,128]{3,2,1,0:T(4,128)S(1)})) conditional(s32[]{:T(128)} %convert_element_type.36, (f32[1,16,128]{2,1,0:T(8,128)S(1)}, f32[1,16,128]{2,1,0:T(8,128)S(1)}, ...), branch_computations={%region_5.5_spmd, %region_6.9_spmd} | conditional | flops 2437986304 | bytes 102952616 | solution.py:105
  154.0 15.7 %conditional.2 = ((f32[1,16,128]{2,1,0:T(8,128)S(1)}, f32[1,16,128]{2,1,0:T(8,128)S(1)}, f32[1,16,128,128]{3,2,1,0:T(8,128)}, f32[1,16,4,128,128]{4,3,2,1,0:T(8,128)}, f32[1,16,4,128]{3,2,1,0:T(4,128)S(1)})) conditional(s32[]{:T(128)} %convert_element_type.36, (f32[1,16,128]{2,1,0:T(8,128)S(1)}, f32[1,16,128]{2,1,0:T(8,128)S(1)}, ...), branch_computations={%region_5.5_spmd, %region_6.9_spmd} | conditional | flops 2437986304 | bytes 102952616 | solution.py:105
  171.8 15.7 %conditional.2 = ((f32[1,16,128]{2,1,0:T(8,128)S(1)}, f32[1,16,128]{2,1,0:T(8,128)S(1)}, f32[1,16,128,128]{3,2,1,0:T(8,128)}, f32[1,16,4,128,128]{4,3,2,1,0:T(8,128)}, f32[1,16,4,128]{3,2,1,0:T(4,128)S(1)})) conditional(s32[]{:T(128)} %convert_element_type.36, (f32[1,16,128]{2,1,0:T(8,128)S(1)}, f32[1,16,128]{2,1,0:T(8,128)S(1)}, ...), branch_computations={%region_5.5_spmd, %region_6.9_spmd} | conditional | flops 2437986304 | bytes 102952616 | solution.py:105
  189.5 15.7 %conditional.2 = ((f32[1,16,128]{2,1,0:T(8,128)S(1)}, f32[1,16,128]{2,1,0:T(8,128)S(1)}, f32[1,16,128,128]{3,2,1,0:T(8,128)}, f32[1,16,4,128,128]{4,3,2,1,0:T(8,128)}, f32[1,16,4,128]{3,2,1,0:T(4,128)S(1)})) conditional(s32[]{:T(128)} %convert_element_type.36, (f32[1,16,128]{2,1,0:T(8,128)S(1)}, f32[1,16,128]{2,1,0:T(8,128)S(1)}, ...), branch_computations={%region_5.5_spmd, %region_6.9_spmd} | conditional | flops 2437986304 | bytes 102952616 | solution.py:105
  207.3 15.7 %conditional.2 = ((f32[1,16,128]{2,1,0:T(8,128)S(1)}, f32[1,16,128]{2,1,0:T(8,128)S(1)}, f32[1,16,128,128]{3,2,1,0:T(8,128)}, f32[1,16,4,128,128]{4,3,2,1,0:T(8,128)}, f32[1,16,4,128]{3,2,1,0:T(4,128)S(1)})) conditional(s32[]{:T(128)} %convert_element_type.36, (f32[1,16,128]{2,1,0:T(8,128)S(1)}, f32[1,16,128]{2,1,0:T(8,128)S(1)}, ...), branch_computations={%region_5.5_spmd, %region_6.9_spmd} | conditional | flops 2437986304 | bytes 102952616 | solution.py:105
  225.1 15.7 %conditional.2 = ((f32[1,16,128]{2,1,0:T(8,128)S(1)}, f32[1,16,128]{2,1,0:T(8,128)S(1)}, f32[1,16,128,128]{3,2,1,0:T(8,128)}, f32[1,16,4,128,128]{4,3,2,1,0:T(8,128)}, f32[1,16,4,128]{3,2,1,0:T(4,128)S(1)})) conditional(s32[]{:T(128)} %convert_element_type.36, (f32[1,16,128]{2,1,0:T(8,128)S(1)}, f32[1,16,128]{2,1,0:T(8,128)S(1)}, ...), branch_computations={%region_5.5_spmd, %region_6.9_spmd} | conditional | flops 2437986304 | bytes 102952616 | solution.py:105
  242.9 15.7 %conditional.2 = ((f32[1,16,128]{2,1,0:T(8,128)S(1)}, f32[1,16,128]{2,1,0:T(8,128)S(1)}, f32[1,16,128,128]{3,2,1,0:T(8,128)}, f32[1,16,4,128,128]{4,3,2,1,0:T(8,128)}, f32[1,16,4,128]{3,2,1,0:T(4,128)S(1)})) conditional(s32[]{:T(128)} %convert_element_type.36, (f32[1,16,128]{2,1,0:T(8,128)S(1)}, f32[1,16,128]{2,1,0:T(8,128)S(1)}, ...), branch_computations={%region_5.5_spmd, %region_6.9_spmd} | conditional | flops 2437986304 | bytes 102952616 | solution.py:105
  261.4 4.7 %all-to-all-start.3 = ((bf16[128,16,128]{2,1,0:T(8,128)(2,1)}), bf16[128,16,128]{2,1,0:T(8,128)(2,1)S(1)}, u32[]{:S(2)}, u32[]{:S(2)}) async-start(bf16[128,16,128]{2,1,0:T(8,128)(2,1)} %get-tuple-element.330), calls=%async_computation.3 | async-start | bytes 1048576 | tf_op jit(solution)/shard_map/all_to_all | solution.py:146
  266.7 8.4 %fusion.36 = bf16[128,16,4,128]{3,2,1,0:T(4,128)(2,1)} fusion(f32[16,4,128]{1,0,2:T(8,128)S(1)} %copy.102, f32[16,128,128]{2,0,1:T(8,128)S(1)} %get-tuple-element.329, f32[16,128]{0,1:T(8,128)S(1)} %copy.97, f32[1,16,4,128,128]{4,3,2,1,0:T(8,128)} %get-tuple-element.221), kind=kLoop, calls=%fused_computation.48 | loop fusion | flops 4194304 | bytes 7380992 | tf_op jit(solution)/shard_map/reshape | solution.py:142
  276.7 4.2 %all-to-all-start.4 = ((bf16[128,16,4,128]{3,2,1,0:T(4,128)(2,1)}), bf16[128,16,4,128]{3,2,1,0:T(4,128)(2,1)S(1)}, u32[]{:S(2)}, u32[]{:S(2)}) async-start(bf16[128,16,4,128]{3,2,1,0:T(4,128)(2,1)} %fusion.36), calls=%async_computation.4 | async-start | bytes 4194304 | tf_op jit(solution)/shard_map/all_to_all | solution.py:147
  281.7 26.0 %all-to-all-done.4 = bf16[128,16,4,128]{3,2,1,0:T(4,128)(2,1)S(1)} async-done(((bf16[128,16,4,128]{3,2,1,0:T(4,128)(2,1)}), bf16[128,16,4,128]{3,2,1,0:T(4,128)(2,1)S(1)}, u32[]{:S(2)}, u32[]{:S(2)}) %all-to-all-start.4) | async-done | bytes 2097184 | tf_op jit(solution)/shard_map/all_to_all | solution.py:147
  (210 shorter events, 156.2 us)
Async XLA Ops:
  7.2 17.4 %copy-start.6 = (bf16[16,128,128]{2,1,0:T(8,128)(2,1)S(1)}, bf16[16,128,128]{2,1,0:T(8,128)(2,1)}, u32[]{:S(2)}) copy-start(bf16[16,128,128]{2,1,0:T(8,128)(2,1)} %param.11) | copy-start | bytes 1572868
  7.2 83.3 %all-gather.2.cloned.1.call-start = ((), (), s32[]{:S(2)}) async-start(), calls=%async_computation.5 | async-start | bytes 5570560 | tf_op jit(solution)/shard_map/all_gather | solution.py:24
  9.8 19.4 %copy-start.5 = (bf16[16,128,4,128]{3,2,1,0:T(4,128)(2,1)S(1)}, bf16[16,128,4,128]{3,2,1,0:T(4,128)(2,1)}, u32[]{:S(2)}) copy-start(bf16[16,128,4,128]{3,2,1,0:T(4,128)(2,1)} %param.12) | copy-start | bytes 6291460
  25.7 12.5 %all-to-all-start.1 = ((bf16[16,128,128]{2,0,1:T(8,128)(2,1)}), bf16[16,128,128]{2,0,1:T(8,128)(2,1)S(1)}, u32[]{:S(2)}, u32[]{:S(2)}) async-start(bf16[16,128,128]{2,0,1:T(8,128)(2,1)} %copy.87), calls=%async_computation.1 | async-start | bytes 1048576 | tf_op jit(solution)/shard_map/all_to_all | solution.py:43
  31.7 10.2 %copy-start.7 = (s32[32]{0:T(128)S(1)}, s32[32]{0:T(128)}, u32[]{:S(2)}) copy-start(s32[32]{0:T(128)} %param.17) | copy-start | bytes 388
  38.2 37.2 %all-to-all-start.2 = ((bf16[16,128,4,128]{3,2,0,1:T(4,128)(2,1)}), bf16[16,128,4,128]{3,2,0,1:T(4,128)(2,1)S(1)}, u32[]{:S(2)}, u32[]{:S(2)}) async-start(bf16[16,128,4,128]{3,2,0,1:T(4,128)(2,1)} %copy.89), calls=%async_computation.2 | async-start | bytes 4194304 | tf_op jit(solution)/shard_map/all_to_all | solution.py:44
  126.5 2.3 copy-start
  132.1 2.0 copy-start.1
  144.2 2.3 copy-start
  149.9 2.0 copy-start.1
  162.0 2.3 copy-start
  167.7 2.0 copy-start.1
  179.8 2.3 copy-start
  185.5 2.0 copy-start.1
  197.6 2.3 copy-start
  203.2 2.0 copy-start.1
  215.3 2.3 copy-start
  221.0 2.0 copy-start.1
  233.1 2.3 copy-start
  238.8 2.0 copy-start.1
  250.9 2.3 copy-start
  256.6 2.0 copy-start.1
  261.4 15.3 %all-to-all-start.3 = ((bf16[128,16,128]{2,1,0:T(8,128)(2,1)}), bf16[128,16,128]{2,1,0:T(8,128)(2,1)S(1)}, u32[]{:S(2)}, u32[]{:S(2)}) async-start(bf16[128,16,128]{2,1,0:T(8,128)(2,1)} %get-tuple-element.330), calls=%async_computation.3 | async-start | bytes 1048576 | tf_op jit(solution)/shard_map/all_to_all | solution.py:146
  276.7 31.0 %all-to-all-start.4 = ((bf16[128,16,4,128]{3,2,1,0:T(4,128)(2,1)}), bf16[128,16,4,128]{3,2,1,0:T(4,128)(2,1)S(1)}, u32[]{:S(2)}, u32[]{:S(2)}) async-start(bf16[128,16,4,128]{3,2,1,0:T(4,128)(2,1)} %fusion.36), calls=%async_computation.4 | async-start | bytes 4194304 | tf_op jit(solution)/shard_map/all_to_all | solution.py:147
  (17 other events, 18.9 us)
Sparse Core Ops, SparseCore 0:
  24.7 65.7 all-gather.1
where the time goes:
time: 320 us; the launch traced here: 317 us
  matrix products  94.8 us (30%)
  waiting for transfers between devices  78.1 us (24%)
  local copies, waits for them, and re-layouts  64.5 us (20%)
  other arithmetic  23.9 us (7%)
  starting transfers between devices  16.1 us (5%)
  between operations  14.2 us (4%)
  blocking collectives  13.5 us (4%)
  loops' own time  12.1 us (4%)
    all_to_all x1, waiting for transfers between devices, per_device(): lax.all_to_all(query_tangents, 'uly', split_axis=1, concat_axis=0, tiled=...  32.5 us
    dot_general x8, matrix products, update(): jnp.einsum('grqk,kgpd->grpqd', weights_half, value_tan, preferred_element...  26.7 us
    all_to_all x1, waiting for transfers between devices, per_device(): lax.all_to_all(tangent_rows, 'uly', split_axis=0, concat_axis=1, tiled=True)  26 us
    cond x72, local copies, waits for them, and re-layouts  23.5 us
    dot_general x8, matrix products, update(): jnp.einsum('grqd,kgpd->grpqk', query_heads, key_tan, preferred_element_ty...  20.7 us
    dot_general x8, matrix products, update(): jnp.einsum('grpqk,kgd->grpqd', weighted.astype(jnp.bfloat16), value_block...  18.4 us
    dot_general x8, matrix products, update(): jnp.einsum('grqk,kgd->grqd', weights_half, value_block, preferred_element...  15.3 us
    all_to_all x1, blocking collectives, in_one_piece(): lax.all_to_all(both, axis, split_axis=split_dim, concat_axis=concat_dim,...  13.5 us
  transfers between devices with their start and end apart: 5, of which 5 were waited for; matrix products, arithmetic and copies ran while one was open for 5% of the time, Pallas kernels for 0%

commit v1 on v0

--- a/solution.py
+++ b/solution.py
@@ -1,3 +1,4 @@
+import functools
 import math
 import jax
 import jax.numpy as jnp
@@ -6,6 +7,18 @@
 
 HQ = 128
 KVH = 8
+
+
+def unite_panels(packet, dev_axis):
+    local_next = lax.axis_size(dev_axis)
+    shaped = jnp.split(packet, local_next, axis=1)
+    value_now = jnp.stack(shaped, axis=0)
+    passed = lax.all_to_all(value_now, dev_axis, 0, 0)
+    left_arr = jnp.concatenate(passed, axis=0)
+    return left_arr
+
+
+map_detail = functools.partial(unite_panels, dev_axis="uly")
 
 
 def in_one_piece(arrays, axis, split_dim, concat_dim, along):
@@ -41,7 +54,7 @@
 def per_device(queries, query_tangents, keys, key_tangents, values, value_tangents, span_order):
     local_queries, local_tangents = (
         lax.all_to_all(queries, "uly", split_axis=1, concat_axis=0, tiled=True),
-        lax.all_to_all(query_tangents, "uly", split_axis=1, concat_axis=0, tiled=True),
+        map_detail(query_tangents),
     )
     query_rows = local_queries.shape[0]
     span_rows = query_rows // 2

time: 320 us -> 318 us (level)
  local copies, waits for them, and re-layouts: 64.5 us -> 67.9 us
  waiting for transfers between devices: 78.1 us -> 74.7 us
    all_to_all x1, waiting for transfers between devices: 6.52 us -> 2.57 us  [per_device(): lax.all_to_all(queries, 'uly', split_axis=1, concat_axis=0, tiled=True)]
    unnamed x12 -> x16, local copies, waits for them, and re-layouts: 6.55 us -> 8.38 us
  transfers between devices with their start and end apart: 5 -> 5, of which waited for: 5 -> 5; matrix products, arithmetic and copies ran while one was open for 5% -> 7% of each run, Pallas kernels for 0% -> 0%
where the time goes in v1:
time: 318 us; the launch traced here: 316 us
  matrix products  94.8 us (30%)
  waiting for transfers between devices  74.7 us (23%)
  local copies, waits for them, and re-layouts  67.9 us (21%)
  other arithmetic  23.3 us (7%)
  starting transfers between devices  16.8 us (5%)
  between operations  14.2 us (4%)
  blocking collectives  13.5 us (4%)
  loops' own time  10.7 us (3%)
    all_to_all x1, waiting for transfers between devices, unite_panels(): passed = lax.all_to_all(value_now, dev_axis, 0, 0)  33.3 us
    dot_general x8, matrix products, update(): jnp.einsum('grqk,kgpd->grpqd', weights_half, value_tan, preferred_element...  26.7 us
    all_to_all x1, waiting for transfers between devices, per_device(): lax.all_to_all(tangent_rows, 'uly', split_axis=0, concat_axis=1, tiled=True)  26 us
    cond x72, local copies, waits for them, and re-layouts  23.5 us
    dot_general x8, matrix products, update(): jnp.einsum('grqd,kgpd->grpqk', query_heads, key_tan, preferred_element_ty...  20.6 us
    dot_general x8, matrix products, update(): jnp.einsum('grpqk,kgd->grpqd', weighted.astype(jnp.bfloat16), value_block...  18.4 us
    dot_general x8, matrix products, update(): jnp.einsum('grqk,kgd->grqd', weights_half, value_block, preferred_element...  15.3 us
    all_to_all x1, blocking collectives, in_one_piece(): lax.all_to_all(both, axis, split_axis=split_dim, concat_axis=concat_dim,...  13.5 us
  transfers between devices with their start and end apart: 5, of which 5 were waited for; matrix products, arithmetic and copies ran while one was open for 7% of the time, Pallas kernels for 0%

profile of v1, /device:TPU:0, one launch (start us, length us, event | category | flops | bytes accessed | tf_op | source)
XLA Modules:
  0.0 315.8 jit_solution(9763907361583456761)
XLA Ops:
  11.0 13.5 %all_to_all.74 = bf16[16,8,1280]{2,0,1:T(8,128)(2,1)} all-to-all(bf16[16,8,1280]{2,0,1:T(8,128)(2,1)S(1)} %pad_maximum_fusion), channel_id=1, replica_groups=mesh['blk'=16,'uly'=8] {'uly'}, dimensions={1} | all-to-all | bytes 655360 | tf_op jit(solution)/shard_map/all_to_all | solution.py:29
  25.7 3.5 %all-to-all-start.1 = ((bf16[16,128,128]{2,0,1:T(8,128)(2,1)}), bf16[16,128,128]{2,0,1:T(8,128)(2,1)S(1)}, u32[]{:S(2)}, u32[]{:S(2)}) async-start(bf16[16,128,128]{2,0,1:T(8,128)(2,1)} %copy.86), calls=%async_computation.1 | async-start | bytes 1048576 | tf_op jit(solution)/shard_map/all_to_all | solution.py:56
  38.2 4.4 %all-to-all-start.2 = ((bf16[8,16,16,4,128]{4,3,2,1,0:T(4,128)(2,1)}), bf16[8,16,16,4,128]{4,3,2,1,0:T(4,128)(2,1)}, u32[]{:S(2)}, u32[]{:S(2)}) async-start(bf16[8,16,16,4,128]{4,3,2,1,0:T(4,128)(2,1)} %bitcast_dynamic-update-slice_fusion), calls=%async_computation.2 | async-start | bytes 4194304 | tf_op jit(solution)/shard_map/all_to_all | solution.py:16
  43.7 33.3 %all-to-all-done.2 = bf16[8,16,16,4,128]{4,3,2,1,0:T(4,128)(2,1)} async-done(((bf16[8,16,16,4,128]{4,3,2,1,0:T(4,128)(2,1)}), bf16[8,16,16,4,128]{4,3,2,1,0:T(4,128)(2,1)}, u32[]{:S(2)}, u32[]{:S(2)}) %all-to-all-start.2) | async-done | bytes 2097184 | tf_op jit(solution)/shard_map/all_to_all | solution.py:16
  80.0 11.2 %all-gather.2.cloned.1.call-done = bf16[2048,1,1280]{2,0,1:T(8,128)(2,1)} async-done(((bf16[128,1,1280]{2,0,1:T(8,128)(2,1)}), bf16[2048,1,1280]{2,0,1:T(8,128)(2,1)}) %all-gather.2.cloned.1.call-update) | async-done | bytes 5242896 | tf_op jit(solution)/shard_map/all_gather | solution.py:37
  91.2 4.6 %fusion.48 = (bf16[2048,1,512]{2,0,1:T(8,128)(2,1)}, bf16[2048,1,512]{2,0,1:T(8,128)(2,1)}) fusion(bf16[2048,1,1280]{2,0,1:T(8,128)(2,1)} %all-gather.2.cloned.1.call-done), kind=kLoop, calls=%fused_computation.89 | loop fusion | bytes 8388608 | tf_op jit(solution)/shard_map/slice | solution.py:39
  95.8 4.0 %reshape.237 = bf16[8,256,1,4,128]{4,3,1,0,2:T(4,128)(2,1)} reshape(bf16[2048,1,512]{2,0,1:T(8,128)(2,1)} %get-tuple-element.325) | data formatting | bytes 4194304 | tf_op jit(solution)/shard_map/reshape;reshape | solution.py:142
  99.8 4.2 %copy.94 = bf16[8,256,1,4,128]{1,4,3,2,0:T(8,128)(2,1)} copy(bf16[8,256,1,4,128]{4,3,1,0,2:T(4,128)(2,1)} %reshape.237) | data formatting | bytes 4194304 | tf_op jit(solution)/shard_map/while | solution.py:145
  104.0 4.0 %reshape.236 = bf16[8,256,1,4,128]{4,3,1,0,2:T(4,128)(2,1)} reshape(bf16[2048,1,512]{2,0,1:T(8,128)(2,1)} %get-tuple-element.326) | data formatting | bytes 4194304 | tf_op jit(solution)/shard_map/reshape;reshape | solution.py:140
  107.9 3.5 %copy.93 = bf16[8,256,1,4,128]{4,1,3,2,0:T(8,128)(2,1)} copy(bf16[8,256,1,4,128]{4,3,1,0,2:T(4,128)(2,1)} %reshape.236) | data formatting | bytes 4194304 | tf_op jit(solution)/shard_map/while | solution.py:145
  117.1 140.1 %while.18 = (s32[]{:T(128)}, f32[1,16,128]{2,1,0:T(8,128)S(1)}, f32[1,16,128]{2,1,0:T(8,128)S(1)}, f32[1,16,128,128]{3,2,1,0:T(8,128)}, f32[1,16,4,128,128]{4,3,...) while((s32[]{:T(128)}, f32[1,16,128]{2,1,0:T(8,128)S(1)}, ...), condition=%wide.region_10.11_spmd, body=%wide.region_3.10_spmd.sunk | while | flops 2437986560 | bytes 102954992 | solution.py:145
  118.9 15.7 %conditional.2 = ((f32[1,16,128]{2,1,0:T(8,128)S(1)}, f32[1,16,128]{2,1,0:T(8,128)S(1)}, f32[1,16,128,128]{3,2,1,0:T(8,128)}, f32[1,16,4,128,128]{4,3,2,1,0:T(8,128)}, f32[1,16,4,128]{3,2,1,0:T(4,128)S(1)})) conditional(s32[]{:T(128)} %convert_element_type.36, (f32[1,16,128]{2,1,0:T(8,128)S(1)}, f32[1,16,128]{2,1,0:T(8,128)S(1)}, ...), branch_computations={%region_5.5_spmd, %region_6.9_spmd} | conditional | flops 2437986304 | bytes 102952616 | solution.py:118
  136.4 15.7 %conditional.2 = ((f32[1,16,128]{2,1,0:T(8,128)S(1)}, f32[1,16,128]{2,1,0:T(8,128)S(1)}, f32[1,16,128,128]{3,2,1,0:T(8,128)}, f32[1,16,4,128,128]{4,3,2,1,0:T(8,128)}, f32[1,16,4,128]{3,2,1,0:T(4,128)S(1)})) conditional(s32[]{:T(128)} %convert_element_type.36, (f32[1,16,128]{2,1,0:T(8,128)S(1)}, f32[1,16,128]{2,1,0:T(8,128)S(1)}, ...), branch_computations={%region_5.5_spmd, %region_6.9_spmd} | conditional | flops 2437986304 | bytes 102952616 | solution.py:118
  146.8 3.3 %bitcast_add_fusion.1 = f32[1,16,4,128,128]{4,3,2,1,0:T(8,128)S(1)} fusion(f32[16,4,128,128]{3,2,1,0:T(8,128)S(1)} %fusion.1, f32[1,16,4,128,128]{4,3,2,1,0:T(8,128)S(1)} %copy-done, f32[16,128]{1,0:T(8,128)S(1)} %get-tuple-element.313, bf16[8,256,1,4,128]{1,4,3,2,0:T(8,128)(2,1)} %get-tuple-element.190, s32[]{:T(128)} %get-tuple-element.182, ...), kind=kOutput, calls=%fused_computation.2 | convolution fusion | flops 542638080 | bytes 14991872 | tf_op jit(solution)/shard_map/while/body/eval_jaxpr/cond/branch_1_fun/grqk,kgpd->grpqd/dot_general | solution.py:108
  153.9 15.7 %conditional.2 = ((f32[1,16,128]{2,1,0:T(8,128)S(1)}, f32[1,16,128]{2,1,0:T(8,128)S(1)}, f32[1,16,128,128]{3,2,1,0:T(8,128)}, f32[1,16,4,128,128]{4,3,2,1,0:T(8,128)}, f32[1,16,4,128]{3,2,1,0:T(4,128)S(1)})) conditional(s32[]{:T(128)} %convert_element_type.36, (f32[1,16,128]{2,1,0:T(8,128)S(1)}, f32[1,16,128]{2,1,0:T(8,128)S(1)}, ...), branch_computations={%region_5.5_spmd, %region_6.9_spmd} | conditional | flops 2437986304 | bytes 102952616 | solution.py:118
  171.5 15.7 %conditional.2 = ((f32[1,16,128]{2,1,0:T(8,128)S(1)}, f32[1,16,128]{2,1,0:T(8,128)S(1)}, f32[1,16,128,128]{3,2,1,0:T(8,128)}, f32[1,16,4,128,128]{4,3,2,1,0:T(8,128)}, f32[1,16,4,128]{3,2,1,0:T(4,128)S(1)})) conditional(s32[]{:T(128)} %convert_element_type.36, (f32[1,16,128]{2,1,0:T(8,128)S(1)}, f32[1,16,128]{2,1,0:T(8,128)S(1)}, ...), branch_computations={%region_5.5_spmd, %region_6.9_spmd} | conditional | flops 2437986304 | bytes 102952616 | solution.py:118
  189.0 15.7 %conditional.2 = ((f32[1,16,128]{2,1,0:T(8,128)S(1)}, f32[1,16,128]{2,1,0:T(8,128)S(1)}, f32[1,16,128,128]{3,2,1,0:T(8,128)}, f32[1,16,4,128,128]{4,3,2,1,0:T(8,128)}, f32[1,16,4,128]{3,2,1,0:T(4,128)S(1)})) conditional(s32[]{:T(128)} %convert_element_type.36, (f32[1,16,128]{2,1,0:T(8,128)S(1)}, f32[1,16,128]{2,1,0:T(8,128)S(1)}, ...), branch_computations={%region_5.5_spmd, %region_6.9_spmd} | conditional | flops 2437986304 | bytes 102952616 | solution.py:118
  206.5 15.7 %conditional.2 = ((f32[1,16,128]{2,1,0:T(8,128)S(1)}, f32[1,16,128]{2,1,0:T(8,128)S(1)}, f32[1,16,128,128]{3,2,1,0:T(8,128)}, f32[1,16,4,128,128]{4,3,2,1,0:T(8,128)}, f32[1,16,4,128]{3,2,1,0:T(4,128)S(1)})) conditional(s32[]{:T(128)} %convert_element_type.36, (f32[1,16,128]{2,1,0:T(8,128)S(1)}, f32[1,16,128]{2,1,0:T(8,128)S(1)}, ...), branch_computations={%region_5.5_spmd, %region_6.9_spmd} | conditional | flops 2437986304 | bytes 102952616 | solution.py:118
  224.0 15.7 %conditional.2 = ((f32[1,16,128]{2,1,0:T(8,128)S(1)}, f32[1,16,128]{2,1,0:T(8,128)S(1)}, f32[1,16,128,128]{3,2,1,0:T(8,128)}, f32[1,16,4,128,128]{4,3,2,1,0:T(8,128)}, f32[1,16,4,128]{3,2,1,0:T(4,128)S(1)})) conditional(s32[]{:T(128)} %convert_element_type.36, (f32[1,16,128]{2,1,0:T(8,128)S(1)}, f32[1,16,128]{2,1,0:T(8,128)S(1)}, ...), branch_computations={%region_5.5_spmd, %region_6.9_spmd} | conditional | flops 2437986304 | bytes 102952616 | solution.py:118
  241.5 15.7 %conditional.2 = ((f32[1,16,128]{2,1,0:T(8,128)S(1)}, f32[1,16,128]{2,1,0:T(8,128)S(1)}, f32[1,16,128,128]{3,2,1,0:T(8,128)}, f32[1,16,4,128,128]{4,3,2,1,0:T(8,128)}, f32[1,16,4,128]{3,2,1,0:T(4,128)S(1)})) conditional(s32[]{:T(128)} %convert_element_type.36, (f32[1,16,128]{2,1,0:T(8,128)S(1)}, f32[1,16,128]{2,1,0:T(8,128)S(1)}, ...), branch_computations={%region_5.5_spmd, %region_6.9_spmd} | conditional | flops 2437986304 | bytes 102952616 | solution.py:118
  260.0 4.7 %all-to-all-start.3 = ((bf16[128,16,128]{2,1,0:T(8,128)(2,1)}), bf16[128,16,128]{2,1,0:T(8,128)(2,1)S(1)}, u32[]{:S(2)}, u32[]{:S(2)}) async-start(bf16[128,16,128]{2,1,0:T(8,128)(2,1)} %get-tuple-element.330), calls=%async_computation.3 | async-start | bytes 1048576 | tf_op jit(solution)/shard_map/all_to_all | solution.py:159
  265.3 8.4 %fusion.36 = bf16[128,16,4,128]{3,2,1,0:T(4,128)(2,1)} fusion(f32[16,4,128]{1,0,2:T(8,128)S(1)} %copy.100, f32[16,128,128]{2,0,1:T(8,128)S(1)} %get-tuple-element.329, f32[16,128]{0,1:T(8,128)S(1)} %copy.95, f32[1,16,4,128,128]{4,3,2,1,0:T(8,128)} %get-tuple-element.221), kind=kLoop, calls=%fused_computation.48 | loop fusion | flops 4194304 | bytes 7380992 | tf_op jit(solution)/shard_map/reshape | solution.py:155
  275.3 4.2 %all-to-all-start.4 = ((bf16[128,16,4,128]{3,2,1,0:T(4,128)(2,1)}), bf16[128,16,4,128]{3,2,1,0:T(4,128)(2,1)S(1)}, u32[]{:S(2)}, u32[]{:S(2)}) async-start(bf16[128,16,4,128]{3,2,1,0:T(4,128)(2,1)} %fusion.36), calls=%async_computation.4 | async-start | bytes 4194304 | tf_op jit(solution)/shard_map/all_to_all | solution.py:160
  280.3 26.0 %all-to-all-done.4 = bf16[128,16,4,128]{3,2,1,0:T(4,128)(2,1)S(1)} async-done(((bf16[128,16,4,128]{3,2,1,0:T(4,128)(2,1)}), bf16[128,16,4,128]{3,2,1,0:T(4,128)(2,1)S(1)}, u32[]{:S(2)}, u32[]{:S(2)}) %all-to-all-start.4) | async-done | bytes 2097184 | tf_op jit(solution)/shard_map/all_to_all | solution.py:160
  (215 shorter events, 158.1 us)
Async XLA Ops:
  7.2 17.4 %copy-start.5 = (bf16[16,128,128]{2,1,0:T(8,128)(2,1)S(1)}, bf16[16,128,128]{2,1,0:T(8,128)(2,1)}, u32[]{:S(2)}) copy-start(bf16[16,128,128]{2,1,0:T(8,128)(2,1)} %param.11) | copy-start | bytes 1572868
  7.2 84.0 %all-gather.2.cloned.1.call-start = ((), (), s32[]{:S(2)}) async-start(), calls=%async_computation.5 | async-start | bytes 5570560 | tf_op jit(solution)/shard_map/all_gather | solution.py:37
  9.8 19.4 %copy-start.4 = (bf16[16,128,4,128]{3,2,1,0:T(4,128)(2,1)S(1)}, bf16[16,128,4,128]{3,2,1,0:T(4,128)(2,1)}, u32[]{:S(2)}) copy-start(bf16[16,128,4,128]{3,2,1,0:T(4,128)(2,1)} %param.12) | copy-start | bytes 6291460
  25.7 12.5 %all-to-all-start.1 = ((bf16[16,128,128]{2,0,1:T(8,128)(2,1)}), bf16[16,128,128]{2,0,1:T(8,128)(2,1)S(1)}, u32[]{:S(2)}, u32[]{:S(2)}) async-start(bf16[16,128,128]{2,0,1:T(8,128)(2,1)} %copy.86), calls=%async_computation.1 | async-start | bytes 1048576 | tf_op jit(solution)/shard_map/all_to_all | solution.py:56
  35.7 7.0 %copy-start.6 = (s32[32]{0:T(128)S(1)}, s32[32]{0:T(128)}, u32[]{:S(2)}) copy-start(s32[32]{0:T(128)} %param.17) | copy-start | bytes 388
  38.2 38.8 %all-to-all-start.2 = ((bf16[8,16,16,4,128]{4,3,2,1,0:T(4,128)(2,1)}), bf16[8,16,16,4,128]{4,3,2,1,0:T(4,128)(2,1)}, u32[]{:S(2)}, u32[]{:S(2)}) async-start(bf16[8,16,16,4,128]{4,3,2,1,0:T(4,128)(2,1)} %bitcast_dynamic-update-slice_fusion), calls=%async_computation.2 | async-start | bytes 4194304 | tf_op jit(solution)/shard_map/all_to_all | solution.py:16
  127.0 2.3 copy-start
  132.6 1.9 copy-start.1
  144.5 2.3 copy-start
  150.1 1.9 copy-start.1
  162.0 2.3 copy-start
  167.7 1.9 copy-start.1
  179.5 2.3 copy-start
  185.2 1.9 copy-start.1
  197.0 2.3 copy-start
  202.7 1.9 copy-start.1
  214.5 2.3 copy-start
  220.2 1.9 copy-start.1
  232.0 2.3 copy-start
  237.7 1.9 copy-start.1
  249.5 2.3 copy-start
  255.2 1.9 copy-start.1
  260.0 15.2 %all-to-all-start.3 = ((bf16[128,16,128]{2,1,0:T(8,128)(2,1)}), bf16[128,16,128]{2,1,0:T(8,128)(2,1)S(1)}, u32[]{:S(2)}, u32[]{:S(2)}) async-start(bf16[128,16,128]{2,1,0:T(8,128)(2,1)} %get-tuple-element.330), calls=%async_computation.3 | async-start | bytes 1048576 | tf_op jit(solution)/shard_map/all_to_all | solution.py:159
  275.3 31.0 %all-to-all-start.4 = ((bf16[128,16,4,128]{3,2,1,0:T(4,128)(2,1)}), bf16[128,16,4,128]{3,2,1,0:T(4,128)(2,1)S(1)}, u32[]{:S(2)}, u32[]{:S(2)}) async-start(bf16[128,16,4,128]{3,2,1,0:T(4,128)(2,1)} %fusion.36), calls=%async_computation.4 | async-start | bytes 4194304 | tf_op jit(solution)/shard_map/all_to_all | solution.py:160
  (16 other events, 17.6 us)
Sparse Core Ops, SparseCore 0:
  24.7 66.4 all-gather.1
